TPU v7x, 32 devices: a whole 2x2x4 slice. The times are simulated.
32 devices in a mesh: row: 4 (over z), col: 8 (over y, x, core).
Axes of the slice: x: 2, y: 2, z: 4, core: 2. Of those that a mesh axis runs over, the one named last changes fastest.
Arguments:
- node_latent: bfloat16 [32768, 128], P(('row', 'col')), may hold values from -6 to 6
- edge_latent: bfloat16 [131072, 128], P(('row', 'col')), may hold values from -6 to 6
- senders: int32 [131072], P(('row', 'col')), may hold values from 0 to 1535
- receivers: int32 [131072], P(('row', 'col')), may hold values from 0 to 1023
- send_index: int32 [32, 4, 128], P(('row', 'col')), may hold values from 0 to 1023
- context_table: bfloat16 [256, 128], P(('row', 'col')), may hold values from -6 to 6
- region: int32 [32768], P(('row', 'col')), may hold values from 0 to 255
- edge_w1: bfloat16 [2, 384, 128], replicated, may hold values from -0.3125 to 0.3125
- edge_w2: bfloat16 [2, 128, 128], replicated, may hold values from -0.5 to 0.5
- edge_bias: float32 [2, 3, 128], replicated, may hold values from -3 to 3
- edge_gain: float32 [2, 128], replicated, may hold values from 0.25 to 1.75
- node_w1: bfloat16 [2, 384, 128], replicated, may hold values from -0.3125 to 0.3125
- node_wg: bfloat16 [2, 128, 128], replicated, may hold values from -0.5 to 0.5
- node_w2: bfloat16 [2, 128, 128], replicated, may hold values from -0.5 to 0.5
- node_bias: float32 [2, 3, 128], replicated, may hold values from -3 to 3
- node_gain: float32 [2, 128], replicated, may hold values from 0.25 to 1.75
Outputs:
- node_out: bfloat16 [32768, 128], P(('row', 'col'))
- edge_out: bfloat16 [131072, 128], P(('row', 'col'))
Inputs may be any that keep to these rules, and one draw needn't show every extreme that they name: senders index the extended table of the edge's own partition: below 1024 its own nodes, then the four received blocks of 128 rows in the order above, below, left, right. receivers are nodes of the edge's own partition. `send_index`: rows of the sending partition's own nodes; repeats may occur.
All inputs are finite; a program needn't handle non-finite values.
Results may differ from a plain program's by a relative error of at most 0.0085.
Values may be sent and summed in bfloat16 or wider, within the bound.
A program may use at most 64 MiB of HBM per device.

v0:
```python
import functools
import math

import jax
import jax.numpy as jnp
from jax import lax
from jax.experimental import pallas as pl
from jax.experimental.pallas import tpu as pltpu
from jax.sharding import PartitionSpec as P

LAYERS = 2
EPS = 1e-05
LANES = 128
BLOCK = 512
F32 = jnp.float32
BF16 = jnp.bfloat16
MESH = pl.DeviceIdType.MESH


def mm(a, b):
    return jnp.dot(a, b, preferred_element_type=F32)


def iota(axis):
    return lax.broadcasted_iota(jnp.int32, (LANES, LANES), axis)


def as_column(row):
    return jnp.transpose(jnp.broadcast_to(row, (LANES, LANES)))


def hot(mask):
    return jnp.where(mask, 1.0, 0.0).astype(BF16)


def pick_parts(index, axis, count):
    base = hot((index & (LANES - 1)) == iota(axis))
    group = (index >> 7).astype(F32).astype(BF16)
    zero = jnp.zeros_like(base)
    return [
        jnp.where(group == jnp.asarray(part, BF16), base, zero) for part in range(count // LANES)
    ]


def pick_rows(column, count):
    return jnp.concatenate(pick_parts(column, 1, count), axis=1)


def centre(values):
    values = values.astype(F32)
    return values - jnp.mean(values, axis=-1, keepdims=True)


def twice(weight):
    zero = jnp.zeros_like(weight)
    top = jnp.concatenate([weight, zero], axis=1)
    return jnp.concatenate([top, jnp.concatenate([zero, weight], axis=1)], axis=0)


def norm(centred, gain, shift):
    spread = jnp.mean(centred * centred, axis=-1, keepdims=True)
    return centred * lax.rsqrt(spread + EPS) * gain + shift


def kernel(
    n_row,
    n_col,
    rest,
    node_ref,
    edge_ref,
    send_ref,
    recv_ref,
    index_ref,
    ctx_ref,
    region_ref,
    ew1,
    ew2,
    eb,
    eg,
    nw1,
    nwg,
    nw2,
    nb,
    ng,
    node_out,
    edge_out,
    hot_send,
    hot_recv,
    hot_sum,
    side_send,
    side_recv,
    hot_index,
    picked,
    halo,
    table,
    from_ext,
    from_own,
    sums,
    ctx_part,
    parts,
    edge_sem,
    halo_send_sem,
    halo_recv_sem,
    row_send_sem,
    row_recv_sem,
    col_send_sem,
    col_recv_sem,
):
    my_row, my_col = lax.axis_index("row"), lax.axis_index("col")
    nodes, width = node_ref.shape
    edges = edge_ref.shape[0]
    count = index_ref.shape[1]
    ext = nodes + 4 * count
    half_ext, half_own = ext // 2, nodes // 2
    ctx_rows = ctx_ref.shape[0]
    edge_in = pltpu.make_async_copy(edge_ref, edge_out, edge_sem)
    edge_in.start()
    per_block = 2 * BLOCK // LANES

    barrier = pltpu.get_barrier_semaphore()
    for step in range(1, n_row):
        pl.semaphore_signal(
            barrier, inc=1, device_id=(lax.rem(my_row + step, n_row), my_col), device_id_type=MESH
        )
    for step in range(1, n_col):
        pl.semaphore_signal(
            barrier, inc=1, device_id=(my_row, lax.rem(my_col + step, n_col)), device_id_type=MESH
        )

    for side in range(4):
        rows = slice(side * count, (side + 1) * count)
        hot_index[rows, :] = pick_rows(as_column(index_ref[side : side + 1, :]), nodes)
    picked[0] = mm(hot_index[...], node_ref[...]).astype(BF16)
    part = jnp.sum(node_ref[...].astype(F32).reshape(nodes // 8, 8, width), axis=0)
    table[my_col, my_row] = jnp.concatenate([ctx_ref[...].astype(F32), part], axis=0)

    pl.semaphore_wait(barrier, n_row + n_col - 2)

    moves = (
        (my_row + 1, my_col, my_row < n_row - 1, my_row > 0),
        (my_row - 1, my_col, my_row > 0, my_row < n_row - 1),
        (my_row, my_col + 1, my_col < n_col - 1, my_col > 0),
        (my_row, my_col - 1, my_col > 0, my_col < n_col - 1),
    )

    def halo_copy(layer, side):
        to_row, to_col = moves[side][:2]
        rows = pl.ds(side * count, count)
        return pltpu.make_async_remote_copy(
            src_ref=picked.at[layer, rows],
            dst_ref=halo.at[layer, rows],
            send_sem=halo_send_sem.at[layer, side],
            recv_sem=halo_recv_sem.at[layer, side],
            device_id=(to_row, to_col),
            device_id_type=MESH,
        )

    def halo_start(layer):
        for side in range(4):

            @pl.when(moves[side][2])
            def _(side=side):
                halo_copy(layer, side).start()

    def halo_wait(layer):
        for side in range(4):

            @pl.when(moves[side][3])
            def _(side=side):
                halo_copy(layer, side).wait_recv()

            @pl.when(jnp.logical_not(moves[side][3]))
            def _(side=side):
                halo[layer, side * count : (side + 1) * count] = jnp.zeros((count, width), BF16)

    def row_copy(step, owner):
        return pltpu.make_async_remote_copy(
            src_ref=table.at[my_col, owner],
            dst_ref=table.at[my_col, owner],
            send_sem=row_send_sem.at[step - 1],
            recv_sem=row_recv_sem.at[step - 1],
            device_id=(lax.rem(my_row + step, n_row), my_col),
            device_id_type=MESH,
        )

    def col_copy(step, owner):
        return pltpu.make_async_remote_copy(
            src_ref=table.at[owner],
            dst_ref=table.at[owner],
            send_sem=col_send_sem.at[step - 1],
            recv_sem=col_recv_sem.at[step - 1],
            device_id=(my_row, lax.rem(my_col + step, n_col)),
            device_id_type=MESH,
        )

    halo_start(0)
    for step in range(1, n_row):
        row_copy(step, my_row).start()
    for copy in rest:
        copy.wait()

    def prepare(block, carry):
        for sub in range(per_block):
            line = block * per_block + sub
            send_row = send_ref[pl.ds(line, 1), :]
            recv_row = recv_ref[pl.ds(line, 1), :]
            rows = pl.ds(pl.multiple_of(line * LANES, LANES), LANES)
            both = as_column(send_row + (recv_row << 16))
            send, recv = both & 0xFFFF, both >> 16
            send_high = (send >= half_ext).astype(jnp.int32)
            side_send[rows, :] = send_high
            recv_high = (recv >= half_own).astype(jnp.int32)
            side_recv[rows, :] = recv_high
            hot_send[rows, :] = pick_rows(send - send_high * half_ext, half_ext)
            hot_recv[rows, :] = pick_rows(recv - recv_high * half_own, half_own)
            recv_low = recv_row - (recv_row >= half_own).astype(jnp.int32) * half_own
            recv_low = jnp.broadcast_to(recv_low, (LANES, LANES))
            for part, value in enumerate(pick_parts(recv_low, 0, half_own)):
                hot_sum[
                    block, part * LANES : (part + 1) * LANES, sub * LANES : (sub + 1) * LANES
                ] = value
        return carry

    lax.fori_loop(0, edges // (2 * BLOCK), prepare, 0)

    for step in range(1, n_row):
        row_copy(step, lax.rem(my_row + n_row - step, n_row)).wait_recv()
    for step in range(1, n_col):
        col_copy(step, my_col).start()

    def fill_own(layer, now):
        w_pair = jnp.concatenate([ew1[layer, :width], ew1[layer, width : 2 * width]], axis=1)
        both = mm(now[...], w_pair).astype(BF16)
        from_ext[:, :width] = both[:half_ext, :width]
        from_ext[: nodes - half_ext, width:] = both[half_ext:, :width]
        from_own[:, :width] = both[:half_own, width:]
        from_own[:, width:] = both[half_own:, width:]

    def edge_phase(layer):
        from_ext[nodes - half_ext :, width:] = mm(halo[layer], ew1[layer, :width]).astype(BF16)
        sums[...] = jnp.zeros_like(sums)
        parts[...] = jnp.zeros_like(parts)
        w_edge = twice(ew1[layer, 2 * width :])
        w_out = twice(centre(ew2[layer]).astype(BF16))
        b_in = eb[0, layer : layer + 1]
        b_out = centre(eb[1, layer : layer + 1])

        def scatter(pair):
            sums[...] += mm(hot_sum[pair], parts[...])

        def body(pair, carry):
            blocks = [
                pl.ds(pl.multiple_of((2 * pair + half) * BLOCK, BLOCK), BLOCK) for half in range(2)
            ]
            old = [edge_out[rows, :] for rows in blocks]
            by_edge = mm(jnp.concatenate(old, axis=1), w_edge)
            by_send = [mm(hot_send[rows, :], from_ext[...]) for rows in blocks]
            by_recv = [mm(hot_recv[rows, :], from_own[...]) for rows in blocks]
            scatter(jnp.maximum(pair - 1, 0))
            hidden = []
            for half, rows in enumerate(blocks):
                pre = by_edge[:, half * width : (half + 1) * width] + b_in
                pre += jnp.where(
                    side_send[rows, :] > 0, by_send[half][:, width:], by_send[half][:, :width]
                )
                pre += jnp.where(
                    side_recv[rows, :] > 0, by_recv[half][:, width:], by_recv[half][:, :width]
                )
                hidden.append(jnp.maximum(pre, 0.0).astype(BF16))
            y_val = mm(jnp.concatenate(hidden, axis=1), w_out)
            for half, rows in enumerate(blocks):
                centred = y_val[:, half * width : (half + 1) * width] + b_out
                new = old[half].astype(F32)
                new += norm(centred, eg[layer : layer + 1], eb[2, layer : layer + 1])
                edge_out[rows, :] = new.astype(BF16)
                high = side_recv[rows, :] > 0
                place = slice(half * BLOCK, (half + 1) * BLOCK)
                parts[place, :width] = jnp.where(high, 0.0, new).astype(BF16)
                parts[place, width:] = jnp.where(high, new, 0.0).astype(BF16)
            return carry

        pairs = edges // (2 * BLOCK)
        lax.fori_loop(0, pairs, body, 0)
        scatter(pairs - 1)

    def node_phase(layer, now, shift_in):
        summed = jnp.concatenate([sums[:, :width], sums[:, width:]], axis=0).astype(BF16)
        feats = jnp.concatenate([now[...], summed], axis=1)
        pre = mm(feats, nw1[layer, : 2 * width]) + shift_in
        pre += ctx_part[:, layer * width : (layer + 1) * width]
        hidden = jnp.maximum(pre, 0.0).astype(BF16)
        centred = mm(hidden, centre(nw2[layer]).astype(BF16)) + centre(nb[1, layer : layer + 1])
        new = now[...].astype(F32)
        new += norm(centred, ng[layer : layer + 1], nb[2, layer : layer + 1])
        node_out[...] = new.astype(BF16)

    fill_own(0, node_ref)
    halo_wait(0)
    edge_in.wait()
    edge_phase(0)

    for step in range(1, n_col):
        col_copy(step, lax.rem(my_col + n_col - step, n_col)).wait_recv()
    pooled_sum = jnp.zeros((8, width), F32)
    shared = []
    for row in range(n_row):
        for col in range(n_col):
            shared.append(table[col, row, :ctx_rows])
            pooled_sum += table[col, row, ctx_rows:]
    pooled = jnp.sum(pooled_sum, axis=0, keepdims=True) / math.sqrt(nodes * n_row * n_col)
    regions = n_row * n_col * ctx_rows
    w_pair = jnp.concatenate([nw1[l, 2 * width :] for l in range(LAYERS)], axis=1)
    projected = mm(jnp.concatenate(shared, axis=0).astype(BF16), w_pair).astype(BF16)
    for line in range(nodes // LANES):
        picker = pick_rows(as_column(region_ref[line : line + 1, :]), regions)
        ctx_part[line * LANES : (line + 1) * LANES, :] = mm(picker, projected)
    def shift_of(layer):
        weight = nwg[layer].astype(F32)
        term = jnp.dot(
            pooled, weight, precision=lax.Precision.HIGHEST, preferred_element_type=F32
        )
        return nb[0, layer : layer + 1] + term

    node_phase(0, node_ref, shift_of(0))

    picked[1] = mm(hot_index[...], node_out[...]).astype(BF16)
    halo_start(1)
    fill_own(1, node_out)
    last_shift = shift_of(1)
    halo_wait(1)
    edge_phase(1)
    node_phase(1, node_out, last_shift)

    for layer in range(LAYERS):
        for side in range(4):

            @pl.when(moves[side][2])
            def _(layer=layer, side=side):
                halo_copy(layer, side).wait_send()

    for step in range(1, n_row):
        row_copy(step, my_row).wait_send()
    for step in range(1, n_col):
        col_copy(step, my_col).wait_send()


EARLY = (0, 4, 5)


def entry(n_row, n_col, count, *refs):
    given, others = refs[:count], list(refs[count : -count])
    held, copy_sem = refs[-count:-1], refs[-1]
    places = list(held)
    places.insert(1, None)
    copies = {
        k: pltpu.make_async_copy(given[k], places[k], copy_sem.at[k])
        for k in range(count)
        if k != 1
    }
    order = EARLY + tuple(k for k in copies if k not in EARLY)
    for k in order:
        copies[k].start()
    for k in EARLY:
        copies[k].wait()
    places[1] = given[1]
    rest = [copies[k] for k in order if k not in EARLY]
    kernel(n_row, n_col, rest, *places, *others)


def local(n_row, n_col, *args):
    node, edge, send, recv, index, ctx, region = args[:7]
    nodes, width = node.shape
    edges = edge.shape[0]
    count = index.shape[2]
    half_ext, half_own = (nodes + 4 * count) // 2, nodes // 2
    vmem = pl.BlockSpec(memory_space=pltpu.VMEM)
    dma = pltpu.SemaphoreType.DMA
    operands = (
        node,
        edge,
        send.reshape(edges // LANES, LANES),
        recv.reshape(edges // LANES, LANES),
        index.reshape(4, count),
        ctx,
        region.reshape(nodes // LANES, LANES),
    ) + args[7:]
    operands = tuple(
        jnp.transpose(x, (1, 0, 2)) if x.shape == (LAYERS, 3, width) else x for x in operands
    )
    operands = tuple(pltpu.with_memory_space_constraint(x, pltpu.HBM) for x in operands)
    return pl.pallas_call(
        functools.partial(entry, n_row, n_col, len(operands)),
        out_shape=(
            jax.ShapeDtypeStruct(node.shape, BF16),
            jax.ShapeDtypeStruct(edge.shape, BF16),
        ),
        in_specs=[pl.BlockSpec(memory_space=pltpu.HBM)] * len(operands),
        out_specs=(vmem, vmem),
        scratch_shapes=[
            pltpu.VMEM((edges, half_ext), BF16),
            pltpu.VMEM((edges, half_own), BF16),
            pltpu.VMEM((edges // (2 * BLOCK), half_own, 2 * BLOCK), BF16),
            pltpu.VMEM((edges, width), jnp.int32),
            pltpu.VMEM((edges, width), jnp.int32),
            pltpu.VMEM((4 * count, nodes), BF16),
            pltpu.VMEM((LAYERS, 4 * count, width), BF16),
            pltpu.VMEM((LAYERS, 4 * count, width), BF16),
            pltpu.VMEM((n_col, n_row, ctx.shape[0] + 8, width), F32),
            pltpu.VMEM((half_ext, 2 * width), BF16),
            pltpu.VMEM((half_own, 2 * width), BF16),
            pltpu.VMEM((half_own, 2 * width), F32),
            pltpu.VMEM((nodes, LAYERS * width), F32),
            pltpu.VMEM((2 * BLOCK, 2 * width), BF16),
            dma(()),
            dma((LAYERS, 4)),
            dma((LAYERS, 4)),
            dma((n_row - 1,)),
            dma((n_row - 1,)),
            dma((n_col - 1,)),
            dma((n_col - 1,)),
        ]
        + [pltpu.VMEM(x.shape, x.dtype) for k, x in enumerate(operands) if k != 1]
        + [dma((len(operands),))],
        compiler_params=pltpu.CompilerParams(
            collective_id=0, has_side_effects=True, vmem_limit_bytes=36 * 1024 * 1024
        ),
        name="mesh_steps",
    )(*operands)


def solution(mesh):
    both = ("row", "col")
    split = (P(both, None), P(both, None), P(both), P(both), P(both, None, None), P(both, None), P(both))
    return jax.shard_map(
        functools.partial(local, mesh.shape["row"], mesh.shape["col"]),
        mesh=mesh,
        in_specs=split + (P(),) * 9,
        out_specs=(P(both, None), P(both, None)),
        check_vma=False,
    )
```

profile of v0, /device:TPU:0, one launch (start us, length us, event | category | flops | bytes accessed | tf_op | source)
XLA Modules:
  0.0 31.9 jit_solution(12133607930697316150)
XLA Ops:
  0.6 29.5 %mesh_steps.1 = (bf16[1024,128]{1,0:T(8,128)(2,1)S(1)}, bf16[4096,128]{1,0:T(8,128)(2,1)S(1)}) custom-call(bf16[1024,128]{1,0:T(8,128)(2,1)} %refs_0_.1, bf16[4096,128]{1,0:T(8,128)(2,1)} %refs_1_.1, s32[32,128]{1,0:T(8,128)} %bitcast.6, s32[32,128]{1,0:T(8,128)} %bitcast.7, s32[4,128]{1,0:T(4,128)} %bitcast.11, bf16[8,128]{1,0:T(8,128)(2,1)} %refs_5_.1, ...), custom_call_target="tpu_custom_call" | custom-call | tf_op jit(solution)/shard_map/mesh_steps/pallas_call | solution.py:391
  30.2 0.7 %copy.20 = bf16[1024,128]{1,0:T(8,128)(2,1)} copy(bf16[1024,128]{1,0:T(8,128)(2,1)S(1)} %get-tuple-element.4) | data formatting | bytes 524288
  30.9 1.0 %copy.21 = bf16[4096,128]{1,0:T(8,128)(2,1)} copy(bf16[4096,128]{1,0:T(8,128)(2,1)S(1)} %get-tuple-element.5) | data formatting | bytes 2097152
where the time goes:
time: 32 us; the launch traced here: 31.9 us
  Pallas kernels  29.5 us (92%)
  local copies, waits for them, and re-layouts  1.67 us (5%)
  between operations  0.65 us (2%)
    pallas_call x1, Pallas kernels, local(): pl.pallas_call(functools.partial(entry, n_row, n_col, len(operands)), out...  29.5 us
    unnamed x2, local copies, waits for them, and re-layouts  1.67 us

commit v1 on v0

v1 whole, which is shorter than its diff:
```python
import functools
import math

import jax
import jax.numpy as jnp
from jax import lax
from jax.experimental import pallas as pl
from jax.experimental.pallas import tpu as pltpu
from jax.sharding import PartitionSpec as P

LAYERS = 2
EPS = 1e-05
LANES = 128
BLOCK = 512
PAIR = 2 * BLOCK
F32 = jnp.float32
BF16 = jnp.bfloat16
I32 = jnp.int32
MESH = pl.DeviceIdType.MESH


def mm(a, b):
    return jnp.dot(a, b, preferred_element_type=F32)


def iota(axis):
    return lax.broadcasted_iota(I32, (LANES, LANES), axis)


def as_column(row):
    return jnp.transpose(jnp.broadcast_to(row, (LANES, LANES)))


def code(index):
    return (LANES + (index & (LANES - 1))) << (index >> 7)


def pick_parts(coded, axis, parts):
    base = (iota(axis) + LANES).astype(F32)
    one, zero = jnp.ones((), BF16), jnp.zeros((), BF16)
    return [
        jnp.where(coded == (base * float(1 << part)).astype(BF16), one, zero) for part in parts
    ]


def pick_rows(coded, parts):
    blocks = []
    for start in range(0, coded.shape[0], LANES):
        blocks.append(jnp.concatenate(pick_parts(coded[start : start + LANES], 1, parts), axis=1))
    return blocks[0] if len(blocks) == 1 else jnp.concatenate(blocks, axis=0)


def centre(values):
    values = values.astype(F32)
    return values - jnp.mean(values, axis=-1, keepdims=True)


def twice(weight):
    zero = jnp.zeros_like(weight)
    top = jnp.concatenate([weight, zero], axis=1)
    return jnp.concatenate([top, jnp.concatenate([zero, weight], axis=1)], axis=0)


def norm(centred, gain, shift):
    width = centred.shape[-1]
    total = jnp.sum(centred * centred, axis=-1, keepdims=True)
    return centred * lax.rsqrt(total + width * EPS) * (gain * math.sqrt(width)) + shift


def fold(ref):
    half = ref.shape[0] // 2
    return jnp.concatenate([ref[:half, :], ref[half:, :]], axis=1)


def kernel(
    n_row,
    n_col,
    early,
    rest,
    node_ref,
    edge_ref,
    send_ref,
    recv_ref,
    index_ref,
    ctx_ref,
    region_ref,
    ew1,
    ew2,
    eb,
    eg,
    nw1,
    nwg,
    nw2,
    nb,
    ng,
    node_out,
    edge_out,
    send_row,
    recv_row,
    send_code,
    recv_code,
    hot_sum,
    hot_index,
    hot_region,
    index_code,
    picked,
    halo,
    table,
    own_send,
    own_recv,
    halo_tab,
    pre_ref,
    sums,
    ctx_part,
    parts,
    edge_sem,
    halo_send_sem,
    halo_recv_sem,
    row_send_sem,
    row_recv_sem,
    col_send_sem,
    col_recv_sem,
    near_row_sem,
    near_col_sem,
    ready_row_sem,
    ready_col_sem,
):
    my_row, my_col = lax.axis_index("row"), lax.axis_index("col")
    devices = n_row * n_col
    nodes, width = node_ref.shape
    edges = edge_ref.shape[0]
    count = index_ref.shape[1]
    half_own, half_halo = nodes // 2, 2 * count
    own_parts = range(half_own // LANES)
    halo_parts = range(half_own // LANES, (half_own + half_halo) // LANES)
    ctx_rows = ctx_ref.shape[0]
    pairs = edges // PAIR

    def in_row(place):
        return (place, my_col)

    def in_col(place):
        return (my_row, place)

    def signal_all(sem, place, low, high):
        def one(other, carry):
            pl.semaphore_signal(sem, inc=1, device_id=place(other), device_id_type=MESH)
            return carry

        lax.fori_loop(low, high, one, 0)

    def wait_for(sem, value):
        @pl.when(value > 0)
        def _():
            pl.semaphore_wait(sem, value)

    edge_in = pltpu.make_async_copy(edge_ref, edge_out, edge_sem)
    edge_in.start()

    moves = (
        (my_row + 1, my_col, my_row < n_row - 1, my_row > 0),
        (my_row - 1, my_col, my_row > 0, my_row < n_row - 1),
        (my_row, my_col + 1, my_col < n_col - 1, my_col > 0),
        (my_row, my_col - 1, my_col > 0, my_col < n_col - 1),
    )
    barrier = pltpu.get_barrier_semaphore()
    signal_all(barrier, in_row, my_row + 1, n_row)
    signal_all(barrier, in_col, my_col + 1, n_col)

    with jax.named_scope("early"):
        for copy in early:
            copy.wait()

    def signed(index, upper):
        return code(index).astype(F32) * jnp.where(upper, -1.0, 1.0)

    sender, receiver = send_ref[...], recv_ref[...]
    in_halo = (sender >= nodes).astype(I32)
    part_size = half_own + (half_halo - half_own) * in_halo
    s_index = sender - nodes * in_halo
    s_upper = s_index >= part_size
    s_index += half_own * in_halo - part_size * s_upper.astype(I32)
    r_upper = receiver >= half_own
    send_row[...] = signed(s_index, s_upper)
    recv_row[...] = signed(receiver - half_own * r_upper.astype(I32), r_upper)

    for line in range(4):
        index = index_ref[line : line + 1, :]
        upper = index >= half_own
        column = as_column(signed(index - half_own * upper.astype(I32), upper))
        rows = slice(line * count, (line + 1) * count)
        index_code[rows, :] = column
        hot_index[rows, :] = pick_rows(jnp.abs(column.astype(BF16)), own_parts)

    def take(coded, both):
        return jnp.where(coded < 0, both[:, width:], both[:, :width])

    def pick(layer, now):
        picked[layer] = take(index_code[...], mm(hot_index[...], fold(now))).astype(BF16)

    pick(0, node_ref)
    part = jnp.sum(node_ref[...].astype(F32).reshape(nodes // 8, 8, width), axis=0)
    left = jnp.sum(part, axis=0, keepdims=True)
    pieces = []
    for _ in range(3):
        pieces.append(left.astype(BF16).astype(F32))
        left = left - pieces[-1]
    block = [ctx_ref[...].astype(F32)] + pieces + [jnp.zeros((5, width), F32)]
    table[my_col, my_row] = jnp.concatenate(block, axis=0).astype(BF16)

    def halo_copy(layer, line):
        rows = pl.ds(line * count, count)
        return pltpu.make_async_remote_copy(
            src_ref=picked.at[layer, rows],
            dst_ref=halo.at[layer, rows],
            send_sem=halo_send_sem.at[layer, line],
            recv_sem=halo_recv_sem.at[layer, line],
            device_id=moves[line][:2],
            device_id_type=MESH,
        )

    def halo_start(layer, lines):
        for line in lines:

            @pl.when(moves[line][2])
            def _(line=line):
                halo_copy(layer, line).start()

    def halo_wait(layer):
        for line in range(4):

            @pl.when(moves[line][3])
            def _(line=line):
                halo_copy(layer, line).wait_recv()

            @pl.when(jnp.logical_not(moves[line][3]))
            def _(line=line):
                halo[layer, line * count : (line + 1) * count] = jnp.zeros((count, width), BF16)

    def row_copy(other):
        return pltpu.make_async_remote_copy(
            src_ref=table.at[my_col, my_row],
            dst_ref=table.at[my_col, my_row],
            send_sem=row_send_sem,
            recv_sem=row_recv_sem,
            device_id=in_row(other),
            device_id_type=MESH,
        )

    def col_copy(other):
        return pltpu.make_async_remote_copy(
            src_ref=table.at[my_col],
            dst_ref=table.at[my_col],
            send_sem=col_send_sem,
            recv_sem=col_recv_sem,
            device_id=in_col(other),
            device_id_type=MESH,
        )

    def start_all(copy, low, high):
        def one(other, carry):
            copy(other).start()
            return carry

        lax.fori_loop(low, high, one, 0)

    def row_total():
        held = table.at[my_col, pl.ds(0, n_row - 1)]
        return pltpu.make_async_remote_copy(
            src_ref=held,
            dst_ref=held,
            send_sem=row_send_sem,
            recv_sem=row_recv_sem,
            device_id=in_row(lax.rem(my_row + 1, n_row)),
            device_id_type=MESH,
        )

    def col_total():
        held = table.at[pl.ds(0, n_col - 1)]
        return pltpu.make_async_remote_copy(
            src_ref=held,
            dst_ref=held,
            send_sem=col_send_sem,
            recv_sem=col_recv_sem,
            device_id=in_col(lax.rem(my_col + 1, n_col)),
            device_id_type=MESH,
        )

    with jax.named_scope("enter"):
        wait_for(barrier, my_row + my_col)

    @pl.when(my_row > 0)
    def _():
        pl.semaphore_signal(near_row_sem, inc=1, device_id=in_row(my_row - 1), device_id_type=MESH)

    @pl.when(my_col > 0)
    def _():
        pl.semaphore_signal(near_col_sem, inc=1, device_id=in_col(my_col - 1), device_id_type=MESH)

    halo_start(0, (1, 3))
    signal_all(ready_row_sem, in_row, 0, my_row)
    start_all(row_copy, 0, my_row)
    signal_all(ready_col_sem, in_col, 0, my_col)

    def near():
        wait_for(near_row_sem, moves[0][2].astype(I32))
        wait_for(near_col_sem, moves[2][2].astype(I32))
        halo_start(0, (0, 2))

    def first_phase():
        wait_for(ready_row_sem, n_row - 1 - my_row)
        start_all(row_copy, my_row + 1, n_row)

    def second_phase():
        row_total().wait_recv()
        wait_for(ready_col_sem, n_col - 1 - my_col)
        start_all(col_copy, 0, my_col)
        start_all(col_copy, my_col + 1, n_col)

    ahead = jnp.logical_and(my_row == 0, my_col < 2)
    near_pair = 1 + ahead.astype(I32)

    for copy in rest:
        copy.wait()
    edge_in.wait()

    def fill_own(layer, now):
        w_pair = jnp.concatenate([ew1[layer, :width], ew1[layer, width : 2 * width]], axis=1)
        both = mm(now[...], w_pair).astype(BF16)
        own_send[...] = jnp.concatenate([both[:half_own, :width], both[half_own:, :width]], axis=1)
        own_recv[...] = jnp.concatenate([both[:half_own, width:], both[half_own:, width:]], axis=1)

    def blocks_of(pair):
        return [
            pl.ds(pl.multiple_of(pair * PAIR + half * BLOCK, BLOCK), BLOCK) for half in range(2)
        ]

    def encode(pair):
        for sub in range(PAIR // LANES):
            line = pair * (PAIR // LANES) + sub
            rows = pl.ds(pl.multiple_of(line * LANES, LANES), LANES)
            recv = recv_row[pl.ds(line, 1), :]
            send_code[rows, :] = as_column(send_row[pl.ds(line, 1), :])
            recv_code[rows, :] = as_column(recv)
            across = jnp.broadcast_to(jnp.abs(recv), (LANES, LANES)).astype(BF16)
            for part, value in enumerate(pick_parts(across, 0, own_parts)):
                hot_sum[
                    pair, part * LANES : (part + 1) * LANES, sub * LANES : (sub + 1) * LANES
                ] = value

    def gather_phase(layer):
        w_edge = twice(ew1[layer, 2 * width :])
        b_in = eb[0, layer : layer + 1]

        def body(pair, carry):
            if layer == 0:

                @pl.when(pair == near_pair)
                def _():
                    near()

                @pl.when(jnp.logical_and(pair == pairs - 1, jnp.logical_not(ahead)))
                def _():
                    first_phase()

                encode(pair)
            blocks = blocks_of(pair)
            by_edge = mm(jnp.concatenate([edge_out[rows, :] for rows in blocks], axis=1), w_edge)
            for half, rows in enumerate(blocks):
                send, recv = send_code[rows, :], recv_code[rows, :]
                by_send = mm(pick_rows(jnp.abs(send.astype(BF16)), own_parts), own_send[...])
                by_recv = mm(pick_rows(jnp.abs(recv.astype(BF16)), own_parts), own_recv[...])
                pre = by_edge[:, half * width : (half + 1) * width] + b_in
                pre += take(send, by_send)
                pre += take(recv, by_recv)
                pre_ref[rows, :] = pre
            return carry

        lax.fori_loop(0, pairs, body, 0)

    def fill_halo(layer):
        rows = mm(halo[layer], ew1[layer, :width]).astype(BF16)
        halo_tab[...] = jnp.concatenate([rows[:half_halo], rows[half_halo:]], axis=1)

    def scatter(pair):
        term = mm(hot_sum[pair], parts[...])
        if pair == 0:
            sums[...] = term
        else:
            sums[...] += term

    def edge_phase(layer, first, last):
        w_out = twice(centre(ew2[layer]).astype(BF16))
        b_out = centre(eb[1, layer : layer + 1])
        for pair in range(first, last):
            starts = [pair * PAIR + half * BLOCK for half in range(2)]
            blocks = [slice(start, start + BLOCK) for start in starts]
            by_halo = [
                mm(pick_rows(jnp.abs(send_code[rows, :].astype(BF16)), halo_parts), halo_tab[...])
                for rows in blocks
            ]
            if pair > 0:
                scatter(pair - 1)
            hidden = []
            for half, rows in enumerate(blocks):
                pre = pre_ref[rows, :] + take(send_code[rows, :], by_halo[half])
                hidden.append(jnp.maximum(pre, 0.0).astype(BF16))
            y_val = mm(jnp.concatenate(hidden, axis=1), w_out)
            for half, rows in enumerate(blocks):
                centred = y_val[:, half * width : (half + 1) * width] + b_out
                new = edge_out[rows, :].astype(F32)
                new += norm(centred, eg[layer : layer + 1], eb[2, layer : layer + 1])
                new = new.astype(BF16)
                edge_out[rows, :] = new
                upper = recv_code[rows, :].astype(BF16) < 0
                held = slice(half * BLOCK, (half + 1) * BLOCK)
                zero = jnp.zeros((), BF16)
                parts[held, :width] = jnp.where(upper, zero, new)
                parts[held, width:] = jnp.where(upper, new, zero)

    def node_phase(layer, now):
        scatter(pairs - 1)
        summed = jnp.concatenate([sums[:, :width], sums[:, width:]], axis=0).astype(BF16)
        feats = jnp.concatenate([now[...], summed], axis=1)
        pre = mm(feats, nw1[layer, : 2 * width])
        pre += ctx_part[:, layer * width : (layer + 1) * width]
        hidden = jnp.maximum(pre, 0.0).astype(BF16)
        centred = mm(hidden, centre(nw2[layer]).astype(BF16)) + centre(nb[1, layer : layer + 1])
        new = now[...].astype(F32)
        new += norm(centred, ng[layer : layer + 1], nb[2, layer : layer + 1])
        node_out[...] = new.astype(BF16)

    def context():
        pieces = jnp.sum(table[:, :, ctx_rows:, :].astype(F32), axis=(0, 1))
        pooled = jnp.sum(pieces, axis=0, keepdims=True) / math.sqrt(nodes * devices)
        pieces = []
        for _ in range(3):
            pieces.append(pooled.astype(BF16).astype(F32))
            pooled = pooled - pieces[-1]
        pieces = jnp.concatenate(pieces + [jnp.zeros((13, width), F32)], axis=0).astype(BF16)
        w_global = jnp.concatenate([nwg[l] for l in range(LAYERS)], axis=1)
        shift = jnp.sum(mm(pieces, w_global), axis=0, keepdims=True)
        shift += jnp.concatenate([nb[0, l : l + 1] for l in range(LAYERS)], axis=1)
        shared = jnp.concatenate(
            [table[col, row, :ctx_rows] for row in range(n_row) for col in range(n_col)], axis=0
        )
        w_pair = jnp.concatenate([nw1[l, 2 * width :] for l in range(LAYERS)], axis=1)
        projected = mm(shared, w_pair).astype(BF16)
        ctx_part[...] = mm(hot_region[...], projected) + shift

    fill_own(0, node_ref)
    with jax.named_scope("gather0"):
        gather_phase(0)
    for line in range(nodes // LANES):
        column = as_column(code(region_ref[line : line + 1, :]).astype(F32))
        hot_region[line * LANES : (line + 1) * LANES, :] = pick_rows(
            column.astype(BF16), range(devices * ctx_rows // LANES)
        )
    with jax.named_scope("halo0"):
        halo_wait(0)
    fill_halo(0)
    edge_phase(0, 0, 1)

    @pl.when(ahead)
    def _():
        first_phase()

    @pl.when(jnp.logical_not(ahead))
    def _():
        second_phase()

    edge_phase(0, 1, 2)

    @pl.when(ahead)
    def _():
        second_phase()

    edge_phase(0, 2, pairs)
    with jax.named_scope("colwait"):
        col_total().wait_recv()
    context()
    node_phase(0, node_ref)
    pick(1, node_out)
    halo_start(1, range(4))
    fill_own(1, node_out)
    with jax.named_scope("gather1"):
        gather_phase(1)
    with jax.named_scope("halo1"):
        halo_wait(1)
    fill_halo(1)
    edge_phase(1, 0, pairs)
    node_phase(1, node_out)

    with jax.named_scope("sends"):
        for layer in range(LAYERS):
            for line in range(4):

                @pl.when(moves[line][2])
                def _(layer=layer, line=line):
                    halo_copy(layer, line).wait_send()

        row_total().wait_send()
        col_total().wait_send()


EARLY = (2, 3, 4, 0, 5)


def entry(n_row, n_col, count, *refs):
    given, others = refs[:count], list(refs[count : -count])
    held, copy_sem = refs[-count:-1], refs[-1]
    places = list(held)
    places.insert(1, None)
    copies = {
        k: pltpu.make_async_copy(given[k], places[k], copy_sem.at[k])
        for k in range(count)
        if k != 1
    }
    order = EARLY + tuple(k for k in copies if k not in EARLY)
    for k in order:
        copies[k].start()
    places[1] = given[1]
    early = [copies[k] for k in EARLY]
    rest = [copies[k] for k in order if k not in EARLY]
    kernel(n_row, n_col, early, rest, *places, *others)


def local(n_row, n_col, *args):
    node, edge, send, recv, index, ctx, region = args[:7]
    nodes, width = node.shape
    edges = edge.shape[0]
    count = index.shape[2]
    devices = n_row * n_col
    half_own, half_halo = nodes // 2, 2 * count
    vmem = pl.BlockSpec(memory_space=pltpu.VMEM)
    dma = pltpu.SemaphoreType.DMA
    operands = (
        node,
        edge,
        send.reshape(edges // LANES, LANES),
        recv.reshape(edges // LANES, LANES),
        index.reshape(4, count),
        ctx,
        region.reshape(nodes // LANES, LANES),
    ) + args[7:]
    operands = tuple(
        jnp.transpose(x, (1, 0, 2)) if x.shape == (LAYERS, 3, width) else x for x in operands
    )
    operands = tuple(pltpu.with_memory_space_constraint(x, pltpu.HBM) for x in operands)
    return pl.pallas_call(
        functools.partial(entry, n_row, n_col, len(operands)),
        out_shape=(
            jax.ShapeDtypeStruct(node.shape, BF16),
            jax.ShapeDtypeStruct(edge.shape, BF16),
        ),
        in_specs=[pl.BlockSpec(memory_space=pltpu.HBM)] * len(operands),
        out_specs=(vmem, vmem),
        scratch_shapes=[
            pltpu.VMEM((edges // LANES, LANES), F32),
            pltpu.VMEM((edges // LANES, LANES), F32),
            pltpu.VMEM((edges, width), F32),
            pltpu.VMEM((edges, width), F32),
            pltpu.VMEM((edges // PAIR, half_own, PAIR), BF16),
            pltpu.VMEM((4 * count, half_own), BF16),
            pltpu.VMEM((nodes, devices * ctx.shape[0]), BF16),
            pltpu.VMEM((4 * count, width), F32),
            pltpu.VMEM((LAYERS, 4 * count, width), BF16),
            pltpu.VMEM((LAYERS, 4 * count, width), BF16),
            pltpu.VMEM((n_col, n_row, ctx.shape[0] + 8, width), BF16),
            pltpu.VMEM((half_own, 2 * width), BF16),
            pltpu.VMEM((half_own, 2 * width), BF16),
            pltpu.VMEM((half_halo, 2 * width), BF16),
            pltpu.VMEM((edges, width), F32),
            pltpu.VMEM((half_own, 2 * width), F32),
            pltpu.VMEM((nodes, LAYERS * width), F32),
            pltpu.VMEM((PAIR, 2 * width), BF16),
            dma(()),
            dma((LAYERS, 4)),
            dma((LAYERS, 4)),
            dma(()),
            dma(()),
            dma(()),
            dma(()),
            pltpu.SemaphoreType.REGULAR,
            pltpu.SemaphoreType.REGULAR,
            pltpu.SemaphoreType.REGULAR,
            pltpu.SemaphoreType.REGULAR,
        ]
        + [pltpu.VMEM(x.shape, x.dtype) for k, x in enumerate(operands) if k != 1]
        + [dma((len(operands),))],
        compiler_params=pltpu.CompilerParams(
            collective_id=0, has_side_effects=True, vmem_limit_bytes=36 * 1024 * 1024
        ),
        name="mesh_steps",
    )(*operands)


def solution(mesh):
    both = ("row", "col")
    split = (P(both, None), P(both, None), P(both), P(both), P(both, None, None), P(both, None), P(both))
    return jax.shard_map(
        functools.partial(local, mesh.shape["row"], mesh.shape["col"]),
        mesh=mesh,
        in_specs=split + (P(),) * 9,
        out_specs=(P(both, None), P(both, None)),
        check_vma=False,
    )
```

time: 32 us -> 24.8 us (0.78)
  Pallas kernels: 29.5 us -> 22.2 us
    pallas_call x1, Pallas kernels: 29.5 us -> 22.2 us  [local(): pl.pallas_call(functools.partial(entry, n_row, n_col, len(operands)), out...]
where the time goes in v1:
time: 24.8 us; the launch traced here: 24.5 us
  Pallas kernels  22.2 us (90%)
  local copies, waits for them, and re-layouts  1.67 us (7%)
  between operations  0.65 us (3%)
    pallas_call x1, Pallas kernels, local(): pl.pallas_call(functools.partial(entry, n_row, n_col, len(operands)), out...  22.2 us
    unnamed x2, local copies, waits for them, and re-layouts  1.67 us

profile of v1, /device:TPU:0, one launch (start us, length us, event | category | flops | bytes accessed | tf_op | source)
XLA Modules:
  0.0 24.5 jit_solution(14379731984931609260)
XLA Ops:
  0.6 22.2 %mesh_steps.1 = (bf16[1024,128]{1,0:T(8,128)(2,1)S(1)}, bf16[4096,128]{1,0:T(8,128)(2,1)S(1)}) custom-call(bf16[1024,128]{1,0:T(8,128)(2,1)} %refs_0_.1, bf16[4096,128]{1,0:T(8,128)(2,1)} %refs_1_.1, s32[32,128]{1,0:T(8,128)} %bitcast.6, s32[32,128]{1,0:T(8,128)} %bitcast.7, s32[4,128]{1,0:T(4,128)} %bitcast.11, bf16[8,128]{1,0:T(8,128)(2,1)} %refs_5_.1, ...), custom_call_target="tpu_custom_call" | custom-call | tf_op jit(solution)/shard_map/mesh_steps/pallas_call | solution.py:550
  22.9 0.7 %copy.20 = bf16[1024,128]{1,0:T(8,128)(2,1)} copy(bf16[1024,128]{1,0:T(8,128)(2,1)S(1)} %get-tuple-element.4) | data formatting | bytes 524288
  23.6 1.0 %copy.21 = bf16[4096,128]{1,0:T(8,128)(2,1)} copy(bf16[4096,128]{1,0:T(8,128)(2,1)S(1)} %get-tuple-element.5) | data formatting | bytes 2097152

commit v2 on v1

v2 whole, which is shorter than its diff:
```python
import functools
import math
import types

import jax
import jax.numpy as jnp
from jax import lax
from jax.experimental import pallas as pl
from jax.experimental.pallas import tpu as pltpu
from jax.sharding import PartitionSpec as P

LAYERS = 2
EPS = 1e-05
LANES = 128
BLOCK = 512
PAIR = 2 * BLOCK
F32 = jnp.float32
BF16 = jnp.bfloat16
I32 = jnp.int32
MESH = pl.DeviceIdType.MESH


def mm(a, b):
    return jnp.dot(a, b, preferred_element_type=F32)


def mm_halves(a, b):
    half = a.shape[0] // 2
    return jnp.concatenate([mm(a[:half], b), mm(a[half:], b)], axis=0)


def iota(axis):
    return lax.broadcasted_iota(I32, (LANES, LANES), axis)


def as_column(row):
    return jnp.transpose(jnp.broadcast_to(row, (LANES, LANES)))


def code(index):
    return (LANES + (index & (LANES - 1))) << (index >> 7)


def pick_parts(coded, axis, parts):
    base = (iota(axis) + LANES).astype(F32)
    one, zero = jnp.ones((), BF16), jnp.zeros((), BF16)
    if axis == 0:
        base = base.astype(BF16)
        masks = [coded * jnp.asarray(0.5**part, BF16) == base for part in parts]
    else:
        masks = [coded == (base * float(1 << part)).astype(BF16) for part in parts]
    return [jnp.where(mask, one, zero) for mask in masks]


def pick_rows(coded, parts):
    blocks = []
    for start in range(0, coded.shape[0], LANES):
        blocks.append(jnp.concatenate(pick_parts(coded[start : start + LANES], 1, parts), axis=1))
    return blocks[0] if len(blocks) == 1 else jnp.concatenate(blocks, axis=0)


def centre(values):
    values = values.astype(F32)
    return values - jnp.mean(values, axis=-1, keepdims=True)


def twice(weight):
    zero = jnp.zeros_like(weight)
    top = jnp.concatenate([weight, zero], axis=1)
    return jnp.concatenate([top, jnp.concatenate([zero, weight], axis=1)], axis=0)


def norm(centred, gain, shift):
    width = centred.shape[-1]
    total = jnp.sum(centred * centred, axis=-1, keepdims=True)
    return centred * lax.rsqrt(total + width * EPS) * (gain * math.sqrt(width)) + shift


def fold(ref):
    half = ref.shape[0] // 2
    return jnp.concatenate([ref[:half, :], ref[half:, :]], axis=1)


def take(coded, both):
    width = both.shape[1] // 2
    return jnp.where(coded < 0, both[:, width:], both[:, :width])


def scatter(at, pair):
    own_parts = range(at.sums.shape[0] // LANES)
    blocks = []
    for line in range(pair * PAIR // LANES, (pair + 1) * PAIR // LANES):
        coded = jnp.broadcast_to(jnp.abs(at.recv_row[line : line + 1, :]), (LANES, LANES))
        blocks.append(jnp.concatenate(pick_parts(coded.astype(BF16), 0, own_parts), axis=0))
    term = mm_halves(jnp.concatenate(blocks, axis=1), at.parts[pair % 2])
    if pair == 0:
        at.sums[...] = term
    else:
        at.sums[...] += term


def edge_phase(at, layer, old_ref, new_ref, ew1=None, done=None):
    edges, width = old_ref.shape
    half_own, half_halo = at.sums.shape[0], at.halo_tab.shape[0]
    pairs = edges // PAIR
    halo_parts = range(half_own // LANES, (half_own + half_halo) // LANES)
    w_out = twice(centre(at.ew2[layer]).astype(BF16))
    b_out = centre(at.eb[1, layer : layer + 1])
    if ew1 is not None:
        w_next = twice(ew1[layer + 1, 2 * width :])

    def blocks_of(pair):
        starts = [pair * PAIR + half * BLOCK for half in range(2)]
        return [slice(start, start + BLOCK) for start in starts]

    def columns(half):
        return slice(half * width, (half + 1) * width)

    def begin(pair):
        hidden = []
        for rows in blocks_of(pair):
            send = at.send_code[rows, :]
            hot = pick_rows(jnp.abs(send.astype(BF16)), halo_parts)
            pre = at.pre_ref[rows, :] + take(send, mm(hot, at.halo_tab[...]))
            hidden.append(jnp.maximum(pre.astype(BF16), jnp.zeros((), BF16)))
        at.y_ref[pair % 2] = mm_halves(jnp.concatenate(hidden, axis=1), w_out)

    def finish(pair):
        for half, rows in enumerate(blocks_of(pair)):
            centred = at.y_ref[pair % 2, :, columns(half)] + b_out
            new = old_ref[rows, :].astype(F32)
            new += norm(centred, at.eg[layer : layer + 1], at.eb[2, layer : layer + 1])
            new = new.astype(BF16)
            new_ref[rows, :] = new
            upper = at.recv_code[rows, :].astype(BF16) < 0
            held = slice(half * BLOCK, (half + 1) * BLOCK)
            zero = jnp.zeros((), BF16)
            at.parts[pair % 2, held, :width] = jnp.where(upper, zero, new)
            at.parts[pair % 2, held, width:] = jnp.where(upper, new, zero)

    def carry_on(pair):
        if ew1 is not None:
            news = [new_ref[rows, :] for rows in blocks_of(pair)]
            by_edge = mm(jnp.concatenate(news, axis=1), w_next)
            for half, rows in enumerate(blocks_of(pair)):
                at.pre_ref[rows, :] = by_edge[:, columns(half)] + at.eb[0, layer + 1 : layer + 2]

    for step in range(pairs + 1):
        if step < pairs:
            begin(step)
        if step > 1:
            scatter(at, step - 2)
            carry_on(step - 2)
        if step > 0:
            finish(step - 1)
        if done is not None and step > 1:
            done(step - 2)
    carry_on(pairs - 1)


def node_begin(at, layer, now):
    width = now.shape[1]
    scatter(at, at.recv_row.shape[0] * LANES // PAIR - 1)
    summed = jnp.concatenate([at.sums[:, :width], at.sums[:, width:]], axis=0).astype(BF16)
    feats = jnp.concatenate([now[...], summed], axis=1)
    return mm_halves(feats, at.nw1[layer, : 2 * width])


def node_end(at, layer, now, pre, new_ref):
    width = now.shape[1]
    pre += at.ctx_part[:, layer * width : (layer + 1) * width]
    hidden = jnp.maximum(pre, 0.0).astype(BF16)
    w_out, b_out = centre(at.nw2[layer]).astype(BF16), centre(at.nb[1, layer : layer + 1])
    new = now[...].astype(F32)
    new += norm(mm_halves(hidden, w_out) + b_out, at.ng[layer : layer + 1], at.nb[2, layer : layer + 1])
    new_ref[...] = new.astype(BF16)


def first_kernel(
    n_row,
    n_col,
    early,
    later,
    rest,
    node_ref,
    edge_ref,
    send_ref,
    recv_ref,
    index_ref,
    ctx_ref,
    region_ref,
    ew1,
    nwg,
    edge_sem,
    at,
    node_out,
    edge_out,
    send_row,
    hot_index,
    hot_region,
    index_code,
    picked,
    halo,
    table,
    pool,
    node_pre,
    own_send,
    own_recv,
    halo_send_sem,
    halo_recv_sem,
    row_send_sem,
    row_recv_sem,
    col_send_sem,
    col_recv_sem,
    near_row_sem,
    near_col_sem,
    ready_row_sem,
    ready_col_sem,
):
    my_row, my_col = lax.axis_index("row"), lax.axis_index("col")
    send_code, recv_code, recv_row = at.send_code, at.recv_code, at.recv_row
    halo_tab, pre_ref, ctx_part = at.halo_tab, at.pre_ref, at.ctx_part
    eb, nw1, nb = at.eb, at.nw1, at.nb
    devices = n_row * n_col
    nodes, width = node_ref.shape
    edges = edge_ref.shape[0]
    count = index_ref.shape[1]
    half_own, half_halo = nodes // 2, 2 * count
    own_parts = range(half_own // LANES)
    ctx_rows = ctx_ref.shape[0]
    pairs = edges // PAIR

    def in_row(place):
        return (place, my_col)

    def in_col(place):
        return (my_row, place)

    def signal_all(sem, place, low, high):
        def one(other, carry):
            pl.semaphore_signal(sem, inc=1, device_id=place(other), device_id_type=MESH)
            return carry

        lax.fori_loop(low, high, one, 0)

    def wait_for(sem, value):
        @pl.when(value > 0)
        def _():
            pl.semaphore_wait(sem, value)

    edge_in = pltpu.make_async_copy(edge_ref, edge_out, edge_sem)
    edge_in.start()

    moves = (
        (my_row + 1, my_col, my_row < n_row - 1, my_row > 0),
        (my_row - 1, my_col, my_row > 0, my_row < n_row - 1),
        (my_row, my_col + 1, my_col < n_col - 1, my_col > 0),
        (my_row, my_col - 1, my_col > 0, my_col < n_col - 1),
    )
    barrier = pltpu.get_barrier_semaphore()
    signal_all(barrier, in_row, my_row + 1, n_row)
    signal_all(barrier, in_col, my_col + 1, n_col)

    with jax.named_scope("early"):
        for copy in early:
            copy.wait()

    part = jnp.sum(node_ref[...].astype(F32).reshape(nodes // 8, 8, width), axis=0)
    pool[my_col, my_row] = jnp.sum(part, axis=0, keepdims=True)
    table[my_col, my_row] = ctx_ref[...]

    def halo_copy(layer, line):
        rows = pl.ds(line * count, count)
        return pltpu.make_async_remote_copy(
            src_ref=picked.at[layer, rows],
            dst_ref=halo.at[layer, rows],
            send_sem=halo_send_sem.at[layer, line],
            recv_sem=halo_recv_sem.at[layer, line],
            device_id=moves[line][:2],
            device_id_type=MESH,
        )

    def halo_start(layer, lines):
        for line in lines:

            @pl.when(moves[line][2])
            def _(line=line):
                halo_copy(layer, line).start()

    def halo_wait(layer):
        for line in range(4):

            @pl.when(moves[line][3])
            def _(line=line):
                halo_copy(layer, line).wait_recv()

            @pl.when(jnp.logical_not(moves[line][3]))
            def _(line=line):
                halo[layer, line * count : (line + 1) * count] = jnp.zeros((count, width), BF16)

    def row_copies(other):
        return [
            pltpu.make_async_remote_copy(
                src_ref=ref.at[my_col, my_row],
                dst_ref=ref.at[my_col, my_row],
                send_sem=row_send_sem.at[k],
                recv_sem=row_recv_sem.at[k],
                device_id=in_row(other),
                device_id_type=MESH,
            )
            for k, ref in enumerate((table, pool))
        ]

    def col_copies(other):
        return [
            pltpu.make_async_remote_copy(
                src_ref=ref.at[my_col],
                dst_ref=ref.at[my_col],
                send_sem=col_send_sem.at[k],
                recv_sem=col_recv_sem.at[k],
                device_id=in_col(other),
                device_id_type=MESH,
            )
            for k, ref in enumerate((table, pool))
        ]

    def start_all(copies, low, high):
        def one(other, carry):
            for copy in copies(other):
                copy.start()
            return carry

        lax.fori_loop(low, high, one, 0)

    def row_totals():
        held = [ref.at[my_col, pl.ds(0, n_row - 1)] for ref in (table, pool)]
        return [
            pltpu.make_async_remote_copy(
                src_ref=ref,
                dst_ref=ref,
                send_sem=row_send_sem.at[k],
                recv_sem=row_recv_sem.at[k],
                device_id=in_row(lax.rem(my_row + 1, n_row)),
                device_id_type=MESH,
            )
            for k, ref in enumerate(held)
        ]

    def col_totals():
        held = [ref.at[pl.ds(0, n_col - 1)] for ref in (table, pool)]
        return [
            pltpu.make_async_remote_copy(
                src_ref=ref,
                dst_ref=ref,
                send_sem=col_send_sem.at[k],
                recv_sem=col_recv_sem.at[k],
                device_id=in_col(lax.rem(my_col + 1, n_col)),
                device_id_type=MESH,
            )
            for k, ref in enumerate(held)
        ]

    row_known = jnp.minimum(my_row + 2, n_row)

    def near():
        wait_for(near_row_sem, moves[0][2].astype(I32))
        wait_for(near_col_sem, moves[2][2].astype(I32))
        halo_start(0, (0, 2))
        start_all(row_copies, my_row + 1, row_known)

    def first_phase():
        wait_for(ready_row_sem, n_row - 1 - my_row)
        start_all(row_copies, row_known, n_row)

    def second_phase():
        for copy in row_totals():
            copy.wait_recv()
        wait_for(ready_col_sem, n_col - 1 - my_col)
        start_all(col_copies, 0, my_col)
        start_all(col_copies, my_col + 1, n_col)

    ahead = jnp.logical_and(my_row == 0, my_col < 2)

    def between(pair, half):
        if (pair, half) == (1, 0):

            @pl.when(jnp.logical_not(ahead))
            def _():
                near()

        if (pair, half) == (2, 1):

            @pl.when(ahead)
            def _():
                near()

            @pl.when(jnp.logical_not(ahead))
            def _():
                first_phase()

    with jax.named_scope("enter"):
        wait_for(barrier, my_row + my_col)
    start_all(row_copies, 0, my_row)
    signal_all(ready_row_sem, in_row, 0, my_row)

    @pl.when(my_row > 0)
    def _():
        pl.semaphore_signal(near_row_sem, inc=1, device_id=in_row(my_row - 1), device_id_type=MESH)

    @pl.when(my_col > 0)
    def _():
        pl.semaphore_signal(near_col_sem, inc=1, device_id=in_col(my_col - 1), device_id_type=MESH)

    signal_all(ready_col_sem, in_col, 0, my_col)

    for copy in later:
        copy.wait()

    def signed(index, upper):
        return code(index).astype(F32) * jnp.where(upper, -1.0, 1.0)

    sender, receiver = send_ref[...], recv_ref[...]
    in_halo = (sender >= nodes).astype(I32)
    part_size = half_own + (half_halo - half_own) * in_halo
    s_index = sender - nodes * in_halo
    s_upper = s_index >= part_size
    s_index += half_own * in_halo - part_size * s_upper.astype(I32)
    r_upper = receiver >= half_own
    send_row[...] = signed(s_index, s_upper)
    recv_row[...] = signed(receiver - half_own * r_upper.astype(I32), r_upper)

    for line in range(4):
        index = index_ref[line : line + 1, :]
        upper = index >= half_own
        column = as_column(signed(index - half_own * upper.astype(I32), upper))
        rows = slice(line * count, (line + 1) * count)
        index_code[rows, :] = column
        hot_index[rows, :] = pick_rows(jnp.abs(column.astype(BF16)), own_parts)

    def pick(layer, now):
        picked[layer] = take(index_code[...], mm_halves(hot_index[...], fold(now))).astype(BF16)

    pick(0, node_ref)
    halo_start(0, (1, 3))
    with jax.named_scope("rest"):
        for copy in rest:
            copy.wait()
    edge_in.wait()

    def fill_own(layer, now):
        w_pair = jnp.concatenate([ew1[layer, :width], ew1[layer, width : 2 * width]], axis=1)
        both = mm_halves(now[...], w_pair).astype(BF16)
        own_send[...] = jnp.concatenate([both[:half_own, :width], both[half_own:, :width]], axis=1)
        own_recv[...] = jnp.concatenate([both[:half_own, width:], both[half_own:, width:]], axis=1)

    def encode(pair):
        for sub in range(PAIR // LANES):
            line = pair * (PAIR // LANES) + sub
            rows = slice(line * LANES, (line + 1) * LANES)
            recv = recv_row[line : line + 1, :]
            send_code[rows, :] = as_column(send_row[line : line + 1, :])
            recv_code[rows, :] = as_column(recv)

    def gather_phase(layer):
        if layer == 0:
            w_edge = twice(ew1[layer, 2 * width :])
            b_in = eb[0, layer : layer + 1]

        for pair in range(pairs):
            if layer == 0:
                between(pair, 0)
                encode(pair)
            starts = [pair * PAIR + half * BLOCK for half in range(2)]
            blocks = [slice(start, start + BLOCK) for start in starts]
            if layer == 0:
                old = [edge_out[rows, :] for rows in blocks]
                by_edge = mm(jnp.concatenate(old, axis=1), w_edge)
            for half, rows in enumerate(blocks):
                if layer == 0 and half == 1:
                    between(pair, 1)
                send, recv = send_code[rows, :], recv_code[rows, :]
                by_send = mm(pick_rows(jnp.abs(send.astype(BF16)), own_parts), own_send[...])
                by_recv = mm(pick_rows(jnp.abs(recv.astype(BF16)), own_parts), own_recv[...])
                if layer == 0:
                    pre = by_edge[:, half * width : (half + 1) * width] + b_in
                else:
                    pre = pre_ref[rows, :]
                pre += take(send, by_send)
                pre += take(recv, by_recv)
                pre_ref[rows, :] = pre

    def fill_halo(layer):
        rows = mm_halves(halo[layer], ew1[layer, :width]).astype(BF16)
        halo_tab[...] = jnp.concatenate([rows[:half_halo], rows[half_halo:]], axis=1)

    def context():
        pooled = jnp.zeros((1, width), F32)
        for col in range(n_col):
            for row in range(n_row):
                pooled += pool[col, row]
        pooled = pooled / math.sqrt(nodes * devices)
        pieces = []
        for _ in range(3):
            pieces.append(pooled.astype(BF16).astype(F32))
            pooled = pooled - pieces[-1]
        pieces = jnp.concatenate(pieces + [jnp.zeros((13, width), F32)], axis=0).astype(BF16)
        w_global = jnp.concatenate([nwg[l] for l in range(LAYERS)], axis=1)
        shift = jnp.sum(mm(pieces, w_global), axis=0, keepdims=True)
        shift += jnp.concatenate([nb[0, l : l + 1] for l in range(LAYERS)], axis=1)
        shared = jnp.concatenate(
            [table[col, row] for row in range(n_row) for col in range(n_col)], axis=0
        )
        w_pair = jnp.concatenate([nw1[l, 2 * width :] for l in range(LAYERS)], axis=1)
        projected = mm(shared, w_pair).astype(BF16)
        ctx_part[...] = mm_halves(hot_region[...], projected) + shift

    fill_own(0, node_ref)
    with jax.named_scope("gather0"):
        gather_phase(0)
    for line in range(nodes // LANES):
        column = as_column(code(region_ref[line : line + 1, :]).astype(F32))
        hot_region[line * LANES : (line + 1) * LANES, :] = pick_rows(
            column.astype(BF16), range(devices * ctx_rows // LANES)
        )
    @pl.when(ahead)
    def _():
        first_phase()

    with jax.named_scope("second"):
        second_phase()
    with jax.named_scope("halo0"):
        halo_wait(0)
    fill_halo(0)
    edge_phase(at, 0, edge_out, edge_out, ew1)
    node_pre[...] = node_begin(at, 0, node_ref)
    with jax.named_scope("colwait"):
        for copy in col_totals():
            copy.wait_recv()
    context()
    node_end(at, 0, node_ref, node_pre[...], node_out)
    pick(1, node_out)
    halo_start(1, range(4))
    fill_own(1, node_out)
    with jax.named_scope("gather1"):
        gather_phase(1)
    with jax.named_scope("halo1"):
        halo_wait(1)
    fill_halo(1)

    with jax.named_scope("sends"):
        for layer in range(LAYERS):
            for line in range(4):

                @pl.when(moves[line][2])
                def _(layer=layer, line=line):
                    halo_copy(layer, line).wait_send()

        for copy in row_totals() + col_totals():
            copy.wait_send()


HELD = ("ew2", "eb", "eg", "nw1", "nw2", "nb", "ng")
CARRIED = ("send_code", "recv_code", "recv_row", "halo_tab", "pre_ref", "ctx_part")


def first_entry(n_row, n_col, *refs):
    given, refs = refs[:16], refs[16:]
    outs, refs = refs[: 2 + len(CARRIED) + len(HELD)], refs[2 + len(CARRIED) + len(HELD) :]
    node_out, edge_out = outs[:2]
    at = types.SimpleNamespace(**dict(zip(CARRIED + HELD, outs[2:])))
    at.sums, at.parts, at.y_ref, edge_sem, copy_sem = refs[:5]
    node, send, recv, index, ctx, region, ew1, nwg = refs[5:13]
    places = [node, None, send, recv, index, ctx, region, ew1, at.ew2, at.eb, at.eg]
    places += [at.nw1, nwg, at.nw2, at.nb, at.ng]
    copies = {
        k: pltpu.make_async_copy(given[k], place, copy_sem.at[k])
        for k, place in enumerate(places)
        if place is not None
    }
    groups = (0, 5), (4, 2, 3)
    groups += (tuple(k for k in copies if k not in sum(groups, ())),)
    for k in sum(groups, ()):
        copies[k].start()
    groups = [[copies[k] for k in group] for group in groups]
    places[1] = given[1]
    first_kernel(n_row, n_col, *groups, *places[:8], nwg, edge_sem, at, node_out, edge_out, *refs[13:])


def second_entry(*refs):
    node, edge, refs = refs[0], refs[1], refs[2:]
    count = len(CARRIED) + len(HELD)
    at = types.SimpleNamespace(**dict(zip(CARRIED + HELD, refs[:count])))
    node_out, edge_out, node_new, edge_new, at.sums, at.parts, at.y_ref = refs[count : count + 7]
    node_sem, edge_sem = refs[count + 7 :]
    pairs = edge.shape[0] // PAIR

    def edge_copy(pair):
        rows = pl.ds(pair * PAIR, PAIR)
        return pltpu.make_async_copy(edge_new.at[rows], edge_out.at[rows], edge_sem.at[pair])

    edge_phase(at, 1, edge, edge_new, done=lambda pair: edge_copy(pair).start())
    edge_copy(pairs - 1).start()
    node_end(at, 1, node, node_begin(at, 1, node), node_new)
    node_copy = pltpu.make_async_copy(node_new, node_out, node_sem)
    node_copy.start()
    for pair in range(pairs):
        edge_copy(pair).wait()
    node_copy.wait()


def local(n_row, n_col, *args):
    node, edge, send, recv, index, ctx, region = args[:7]
    nodes, width = node.shape
    edges = edge.shape[0]
    count = index.shape[2]
    devices = n_row * n_col
    half_own, half_halo = nodes // 2, 2 * count
    vmem = pl.BlockSpec(memory_space=pltpu.VMEM)
    hbm = pl.BlockSpec(memory_space=pltpu.HBM)
    dma = pltpu.SemaphoreType.DMA
    operands = (
        node,
        edge,
        send.reshape(edges // LANES, LANES),
        recv.reshape(edges // LANES, LANES),
        index.reshape(4, count),
        ctx,
        region.reshape(nodes // LANES, LANES),
    ) + args[7:]
    operands = tuple(
        jnp.transpose(x, (1, 0, 2)) if x.shape == (LAYERS, 3, width) else x for x in operands
    )
    operands = tuple(pltpu.with_memory_space_constraint(x, pltpu.HBM) for x in operands)
    held = [operands[k] for k in (8, 9, 10, 11, 13, 14, 15)]
    carried = [
        ((edges, width), F32),
        ((edges, width), F32),
        ((edges // LANES, LANES), F32),
        ((half_halo, 2 * width), BF16),
        ((edges, width), F32),
        ((nodes, LAYERS * width), F32),
    ]
    shared = [
        jax.ShapeDtypeStruct(node.shape, BF16),
        jax.ShapeDtypeStruct(edge.shape, BF16),
    ]
    passed = shared + [jax.ShapeDtypeStruct(*x) for x in carried]
    passed += [jax.ShapeDtypeStruct(x.shape, x.dtype) for x in held]
    local_scratch = [
        pltpu.VMEM((half_own, 2 * width), F32),
        pltpu.VMEM((2, PAIR, 2 * width), BF16),
        pltpu.VMEM((2, BLOCK, 2 * width), F32),
    ]
    between = pl.pallas_call(
        functools.partial(first_entry, n_row, n_col),
        out_shape=tuple(passed),
        in_specs=[hbm] * len(operands),
        out_specs=(vmem,) * len(passed),
        scratch_shapes=local_scratch
        + [dma(()), dma((len(operands),))]
        + [pltpu.VMEM(operands[k].shape, operands[k].dtype) for k in (0, 2, 3, 4, 5, 6, 7, 12)]
        + [
            pltpu.VMEM((edges // LANES, LANES), F32),
            pltpu.VMEM((4 * count, half_own), BF16),
            pltpu.VMEM((nodes, devices * ctx.shape[0]), BF16),
            pltpu.VMEM((4 * count, width), F32),
            pltpu.VMEM((LAYERS, 4 * count, width), BF16),
            pltpu.VMEM((LAYERS, 4 * count, width), BF16),
            pltpu.VMEM((n_col, n_row, ctx.shape[0], width), BF16),
            pltpu.VMEM((n_col, n_row, 1, width), F32),
            pltpu.VMEM((nodes, width), F32),
            pltpu.VMEM((half_own, 2 * width), BF16),
            pltpu.VMEM((half_own, 2 * width), BF16),
            dma((LAYERS, 4)),
            dma((LAYERS, 4)),
            dma((2,)),
            dma((2,)),
            dma((2,)),
            dma((2,)),
            pltpu.SemaphoreType.REGULAR,
            pltpu.SemaphoreType.REGULAR,
            pltpu.SemaphoreType.REGULAR,
            pltpu.SemaphoreType.REGULAR,
        ],
        compiler_params=pltpu.CompilerParams(
            collective_id=0, has_side_effects=True, vmem_limit_bytes=24 * 1024 * 1024
        ),
        name="mesh_first",
    )(*operands)
    return pl.pallas_call(
        second_entry,
        out_shape=tuple(shared),
        in_specs=[vmem] * len(passed),
        out_specs=(hbm, hbm),
        scratch_shapes=[pltpu.VMEM(node.shape, BF16), pltpu.VMEM(edge.shape, BF16)]
        + local_scratch
        + [dma(()), dma((edges // PAIR,))],
        compiler_params=pltpu.CompilerParams(vmem_limit_bytes=24 * 1024 * 1024),
        name="mesh_second",
    )(*between)


def solution(mesh):
    both = ("row", "col")
    split = (P(both, None), P(both, None), P(both), P(both), P(both, None, None), P(both, None), P(both))
    return jax.shard_map(
        functools.partial(local, mesh.shape["row"], mesh.shape["col"]),
        mesh=mesh,
        in_specs=split + (P(),) * 9,
        out_specs=(P(both, None), P(both, None)),
        check_vma=False,
    )
```

time: 24.8 us -> 21 us (0.85)
  Pallas kernels: 22.2 us -> 20.1 us
  local copies, waits for them, and re-layouts: 1.67 us -> 0 us
    pallas_call x1 -> x2, Pallas kernels: 22.2 us -> 20.1 us  [the longest x1 16.2 us: local(): pl.pallas_call(functools.partial(first_entry, n_row, n_col), out_shape=tu...]
    unnamed x2 -> x0, local copies, waits for them, and re-layouts: 1.67 us -> none
where the time goes in v2:
time: 21 us; the launch traced here: 20.9 us
  Pallas kernels  20.1 us (96%)
  between operations  0.81 us (4%)
    pallas_call x1, Pallas kernels, local(): pl.pallas_call(functools.partial(first_entry, n_row, n_col), out_shape=tu...  16.2 us
    pallas_call x1, Pallas kernels, local(): pl.pallas_call(second_entry, out_shape=tuple(shared), in_specs=[vmem] * l...  3.83 us

profile of v2, /device:TPU:0, one launch (start us, length us, event | category | flops | bytes accessed | tf_op | source)
XLA Modules:
  0.0 20.9 jit_solution(15968563373101671146)
XLA Ops:
  0.6 16.2 %mesh_first.1 = (bf16[1024,128]{1,0:T(8,128)(2,1)S(1)}, bf16[4096,128]{1,0:T(8,128)(2,1)S(1)}, f32[4096,128]{1,0:T(8,128)S(1)}, f32[4096,128]{1,0:T(8,128)S(1)},...) custom-call(bf16[1024,128]{1,0:T(8,128)(2,1)} %refs_0_.1, ...), custom_call_target="tpu_custom_call" | custom-call | tf_op jit(solution)/shard_map/mesh_first/pallas_call | solution.py:654
  16.9 3.8 %mesh_second.1 = (bf16[1024,128]{1,0:T(8,128)(2,1)}, bf16[4096,128]{1,0:T(8,128)(2,1)}) custom-call(bf16[1024,128]{1,0:T(8,128)(2,1)S(1)} %get-tuple-element.17.refs_0_, bf16[4096,128]{1,0:T(8,128)(2,1)S(1)} %get-tuple-element.18.refs_1_, f32[4096,128]{1,0:T(8,128)S(1)} %get-tuple-element.19.refs_2_, f32[4096,128]{1,0:T(8,128)S(1)} %get-tuple-element.20.refs_3_, ...), custom_call_target="tpu_custom_call" | custom-call | tf_op jit(solution)/shard_map/mesh_second/pallas_call | solution.py:690

commit v3 on v2

--- a/solution.py
+++ b/solution.py
@@ -92,7 +92,7 @@
     for line in range(pair * PAIR // LANES, (pair + 1) * PAIR // LANES):
         coded = jnp.broadcast_to(jnp.abs(at.recv_row[line : line + 1, :]), (LANES, LANES))
         blocks.append(jnp.concatenate(pick_parts(coded.astype(BF16), 0, own_parts), axis=0))
-    term = mm_halves(jnp.concatenate(blocks, axis=1), at.parts[pair % 2])
+    term = mm_halves(jnp.concatenate(blocks, axis=1), at.parts[...])
     if pair == 0:
         at.sums[...] = term
     else:
@@ -135,8 +135,8 @@
             upper = at.recv_code[rows, :].astype(BF16) < 0
             held = slice(half * BLOCK, (half + 1) * BLOCK)
             zero = jnp.zeros((), BF16)
-            at.parts[pair % 2, held, :width] = jnp.where(upper, zero, new)
-            at.parts[pair % 2, held, width:] = jnp.where(upper, new, zero)
+            at.parts[held, :width] = jnp.where(upper, zero, new)
+            at.parts[held, width:] = jnp.where(upper, new, zero)
 
     def carry_on(pair):
         if ew1 is not None:
@@ -156,6 +156,12 @@
         if done is not None and step > 1:
             done(step - 2)
     carry_on(pairs - 1)
+
+
+def fill_halo(halo_tab, halo, weight):
+    rows = mm_halves(halo, weight).astype(BF16)
+    half = rows.shape[0] // 2
+    halo_tab[...] = jnp.concatenate([rows[:half], rows[half:]], axis=1)
 
 
 def node_begin(at, layer, now):
@@ -219,7 +225,7 @@
 ):
     my_row, my_col = lax.axis_index("row"), lax.axis_index("col")
     send_code, recv_code, recv_row = at.send_code, at.recv_code, at.recv_row
-    halo_tab, pre_ref, ctx_part = at.halo_tab, at.pre_ref, at.ctx_part
+    pre_ref, ctx_part = at.pre_ref, at.ctx_part
     eb, nw1, nb = at.eb, at.nw1, at.nb
     devices = n_row * n_col
     nodes, width = node_ref.shape
@@ -294,9 +300,21 @@
             def _(line=line):
                 halo_copy(layer, line).wait_recv()
 
+    def halo_clear():
+        for line in range(4):
+
             @pl.when(jnp.logical_not(moves[line][3]))
             def _(line=line):
-                halo[layer, line * count : (line + 1) * count] = jnp.zeros((count, width), BF16)
+                empty = jnp.zeros((count, width), BF16)
+                for layer in range(LAYERS):
+                    halo[layer, line * count : (line + 1) * count] = empty
+
+    def halo_sent(layer):
+        for line in range(4):
+
+            @pl.when(moves[line][2])
+            def _(line=line):
+                halo_copy(layer, line).wait_send()
 
     def row_copies(other):
         return [
@@ -489,10 +507,6 @@
                 pre += take(recv, by_recv)
                 pre_ref[rows, :] = pre
 
-    def fill_halo(layer):
-        rows = mm_halves(halo[layer], ew1[layer, :width]).astype(BF16)
-        halo_tab[...] = jnp.concatenate([rows[:half_halo], rows[half_halo:]], axis=1)
-
     def context():
         pooled = jnp.zeros((1, width), F32)
         for col in range(n_col):
@@ -526,13 +540,17 @@
     def _():
         first_phase()
 
+    halo_clear()
     with jax.named_scope("second"):
         second_phase()
     with jax.named_scope("halo0"):
         halo_wait(0)
-    fill_halo(0)
+    fill_halo(at.halo_tab, halo[0], ew1[0, :width])
     edge_phase(at, 0, edge_out, edge_out, ew1)
     node_pre[...] = node_begin(at, 0, node_ref)
+    halo_sent(0)
+    for copy in row_totals() + col_totals():
+        copy.wait_send()
     with jax.named_scope("colwait"):
         for copy in col_totals():
             copy.wait_recv()
@@ -545,22 +563,14 @@
         gather_phase(1)
     with jax.named_scope("halo1"):
         halo_wait(1)
-    fill_halo(1)
+    at.halo_last[...] = halo[1]
 
     with jax.named_scope("sends"):
-        for layer in range(LAYERS):
-            for line in range(4):
-
-                @pl.when(moves[line][2])
-                def _(layer=layer, line=line):
-                    halo_copy(layer, line).wait_send()
-
-        for copy in row_totals() + col_totals():
-            copy.wait_send()
-
-
-HELD = ("ew2", "eb", "eg", "nw1", "nw2", "nb", "ng")
-CARRIED = ("send_code", "recv_code", "recv_row", "halo_tab", "pre_ref", "ctx_part")
+        halo_sent(1)
+
+
+HELD = ("ew1", "ew2", "eb", "eg", "nw1", "nw2", "nb", "ng")
+CARRIED = ("send_code", "recv_code", "recv_row", "halo_last", "pre_ref", "ctx_part")
 
 
 def first_entry(n_row, n_col, *refs):
@@ -568,9 +578,9 @@
     outs, refs = refs[: 2 + len(CARRIED) + len(HELD)], refs[2 + len(CARRIED) + len(HELD) :]
     node_out, edge_out = outs[:2]
     at = types.SimpleNamespace(**dict(zip(CARRIED + HELD, outs[2:])))
-    at.sums, at.parts, at.y_ref, edge_sem, copy_sem = refs[:5]
-    node, send, recv, index, ctx, region, ew1, nwg = refs[5:13]
-    places = [node, None, send, recv, index, ctx, region, ew1, at.ew2, at.eb, at.eg]
+    at.sums, at.parts, at.y_ref, at.halo_tab, edge_sem, copy_sem = refs[:6]
+    node, send, recv, index, ctx, region, nwg = refs[6:13]
+    places = [node, None, send, recv, index, ctx, region, at.ew1, at.ew2, at.eb, at.eg]
     places += [at.nw1, nwg, at.nw2, at.nb, at.ng]
     copies = {
         k: pltpu.make_async_copy(given[k], place, copy_sem.at[k])
@@ -591,13 +601,14 @@
     count = len(CARRIED) + len(HELD)
     at = types.SimpleNamespace(**dict(zip(CARRIED + HELD, refs[:count])))
     node_out, edge_out, node_new, edge_new, at.sums, at.parts, at.y_ref = refs[count : count + 7]
-    node_sem, edge_sem = refs[count + 7 :]
+    at.halo_tab, node_sem, edge_sem = refs[count + 7 :]
     pairs = edge.shape[0] // PAIR
 
     def edge_copy(pair):
         rows = pl.ds(pair * PAIR, PAIR)
         return pltpu.make_async_copy(edge_new.at[rows], edge_out.at[rows], edge_sem.at[pair])
 
+    fill_halo(at.halo_tab, at.halo_last[...], at.ew1[1, : edge.shape[1]])
     edge_phase(at, 1, edge, edge_new, done=lambda pair: edge_copy(pair).start())
     edge_copy(pairs - 1).start()
     node_end(at, 1, node, node_begin(at, 1, node), node_new)
@@ -631,12 +642,12 @@
         jnp.transpose(x, (1, 0, 2)) if x.shape == (LAYERS, 3, width) else x for x in operands
     )
     operands = tuple(pltpu.with_memory_space_constraint(x, pltpu.HBM) for x in operands)
-    held = [operands[k] for k in (8, 9, 10, 11, 13, 14, 15)]
+    held = [operands[k] for k in (7, 8, 9, 10, 11, 13, 14, 15)]
     carried = [
         ((edges, width), F32),
         ((edges, width), F32),
         ((edges // LANES, LANES), F32),
-        ((half_halo, 2 * width), BF16),
+        ((4 * count, width), BF16),
         ((edges, width), F32),
         ((nodes, LAYERS * width), F32),
     ]
@@ -648,8 +659,9 @@
     passed += [jax.ShapeDtypeStruct(x.shape, x.dtype) for x in held]
     local_scratch = [
         pltpu.VMEM((half_own, 2 * width), F32),
-        pltpu.VMEM((2, PAIR, 2 * width), BF16),
+        pltpu.VMEM((PAIR, 2 * width), BF16),
         pltpu.VMEM((2, BLOCK, 2 * width), F32),
+        pltpu.VMEM((half_halo, 2 * width), BF16),
     ]
     between = pl.pallas_call(
         functools.partial(first_entry, n_row, n_col),
@@ -658,7 +670,7 @@
         out_specs=(vmem,) * len(passed),
         scratch_shapes=local_scratch
         + [dma(()), dma((len(operands),))]
-        + [pltpu.VMEM(operands[k].shape, operands[k].dtype) for k in (0, 2, 3, 4, 5, 6, 7, 12)]
+        + [pltpu.VMEM(operands[k].shape, operands[k].dtype) for k in (0, 2, 3, 4, 5, 6, 12)]
         + [
             pltpu.VMEM((edges // LANES, LANES), F32),
             pltpu.VMEM((4 * count, half_own), BF16),

time: 21 us -> 20.8 us (level)
    pallas_call x1, Pallas kernels: 16.2 us -> 15.9 us  [local(): pl.pallas_call(functools.partial(first_entry, n_row, n_col), out_shape=tu...]
where the time goes in v3:
time: 20.8 us; the launch traced here: 20.7 us
  Pallas kernels  19.9 us (96%)
  between operations  0.81 us (4%)
    pallas_call x1, Pallas kernels, local(): pl.pallas_call(functools.partial(first_entry, n_row, n_col), out_shape=tu...  15.9 us
    pallas_call x1, Pallas kernels, local(): pl.pallas_call(second_entry, out_shape=tuple(shared), in_specs=[vmem] * l...  3.97 us

profile of v3, /device:TPU:0, one launch (start us, length us, event | category | flops | bytes accessed | tf_op | source)
XLA Modules:
  0.0 20.7 jit_solution(14967173889589220726)
XLA Ops:
  0.6 15.9 %mesh_first.1 = (bf16[1024,128]{1,0:T(8,128)(2,1)S(1)}, bf16[4096,128]{1,0:T(8,128)(2,1)S(1)}, f32[4096,128]{1,0:T(8,128)S(1)}, f32[4096,128]{1,0:T(8,128)S(1)},...) custom-call(bf16[1024,128]{1,0:T(8,128)(2,1)} %refs_0_.1, ...), custom_call_target="tpu_custom_call" | custom-call | tf_op jit(solution)/shard_map/mesh_first/pallas_call | solution.py:666
  16.5 4.0 %mesh_second.1 = (bf16[1024,128]{1,0:T(8,128)(2,1)}, bf16[4096,128]{1,0:T(8,128)(2,1)}) custom-call(bf16[1024,128]{1,0:T(8,128)(2,1)S(1)} %get-tuple-element.18.refs_0_, bf16[4096,128]{1,0:T(8,128)(2,1)S(1)} %get-tuple-element.19.refs_1_, f32[4096,128]{1,0:T(8,128)S(1)} %get-tuple-element.20.refs_2_, f32[4096,128]{1,0:T(8,128)S(1)} %get-tuple-element.21.refs_3_, ...), custom_call_target="tpu_custom_call" | custom-call | tf_op jit(solution)/shard_map/mesh_second/pallas_call | solution.py:702

commit v4 on v3

--- a/solution.py
+++ b/solution.py
@@ -14,6 +14,7 @@
 LANES = 128
 BLOCK = 512
 PAIR = 2 * BLOCK
+STEP = 2048
 F32 = jnp.float32
 BF16 = jnp.bfloat16
 I32 = jnp.int32
@@ -89,7 +90,7 @@
 def scatter(at, pair):
     own_parts = range(at.sums.shape[0] // LANES)
     blocks = []
-    for line in range(pair * PAIR // LANES, (pair + 1) * PAIR // LANES):
+    for line in range(pair * STEP // LANES, (pair + 1) * STEP // LANES):
         coded = jnp.broadcast_to(jnp.abs(at.recv_row[line : line + 1, :]), (LANES, LANES))
         blocks.append(jnp.concatenate(pick_parts(coded.astype(BF16), 0, own_parts), axis=0))
     term = mm_halves(jnp.concatenate(blocks, axis=1), at.parts[...])
@@ -102,7 +103,7 @@
 def edge_phase(at, layer, old_ref, new_ref, ew1=None, done=None):
     edges, width = old_ref.shape
     half_own, half_halo = at.sums.shape[0], at.halo_tab.shape[0]
-    pairs = edges // PAIR
+    pairs = edges // STEP
     halo_parts = range(half_own // LANES, (half_own + half_halo) // LANES)
     w_out = twice(centre(at.ew2[layer]).astype(BF16))
     b_out = centre(at.eb[1, layer : layer + 1])
@@ -110,8 +111,8 @@
         w_next = twice(ew1[layer + 1, 2 * width :])
 
     def blocks_of(pair):
-        starts = [pair * PAIR + half * BLOCK for half in range(2)]
-        return [slice(start, start + BLOCK) for start in starts]
+        starts = [pair * STEP + half * STEP // 2 for half in range(2)]
+        return [slice(start, start + STEP // 2) for start in starts]
 
     def columns(half):
         return slice(half * width, (half + 1) * width)
@@ -133,7 +134,7 @@
             new = new.astype(BF16)
             new_ref[rows, :] = new
             upper = at.recv_code[rows, :].astype(BF16) < 0
-            held = slice(half * BLOCK, (half + 1) * BLOCK)
+            held = slice(half * STEP // 2, (half + 1) * STEP // 2)
             zero = jnp.zeros((), BF16)
             at.parts[held, :width] = jnp.where(upper, zero, new)
             at.parts[held, width:] = jnp.where(upper, new, zero)
@@ -166,7 +167,7 @@
 
 def node_begin(at, layer, now):
     width = now.shape[1]
-    scatter(at, at.recv_row.shape[0] * LANES // PAIR - 1)
+    scatter(at, at.recv_row.shape[0] * LANES // STEP - 1)
     summed = jnp.concatenate([at.sums[:, :width], at.sums[:, width:]], axis=0).astype(BF16)
     feats = jnp.concatenate([now[...], summed], axis=1)
     return mm_halves(feats, at.nw1[layer, : 2 * width])
@@ -602,10 +603,10 @@
     at = types.SimpleNamespace(**dict(zip(CARRIED + HELD, refs[:count])))
     node_out, edge_out, node_new, edge_new, at.sums, at.parts, at.y_ref = refs[count : count + 7]
     at.halo_tab, node_sem, edge_sem = refs[count + 7 :]
-    pairs = edge.shape[0] // PAIR
+    pairs = edge.shape[0] // STEP
 
     def edge_copy(pair):
-        rows = pl.ds(pair * PAIR, PAIR)
+        rows = pl.ds(pair * STEP, STEP)
         return pltpu.make_async_copy(edge_new.at[rows], edge_out.at[rows], edge_sem.at[pair])
 
     fill_halo(at.halo_tab, at.halo_last[...], at.ew1[1, : edge.shape[1]])
@@ -659,8 +660,8 @@
     passed += [jax.ShapeDtypeStruct(x.shape, x.dtype) for x in held]
     local_scratch = [
         pltpu.VMEM((half_own, 2 * width), F32),
-        pltpu.VMEM((PAIR, 2 * width), BF16),
-        pltpu.VMEM((2, BLOCK, 2 * width), F32),
+        pltpu.VMEM((STEP, 2 * width), BF16),
+        pltpu.VMEM((2, STEP // 2, 2 * width), F32),
         pltpu.VMEM((half_halo, 2 * width), BF16),
     ]
     between = pl.pallas_call(
@@ -706,7 +707,7 @@
         out_specs=(hbm, hbm),
         scratch_shapes=[pltpu.VMEM(node.shape, BF16), pltpu.VMEM(edge.shape, BF16)]
         + local_scratch
-        + [dma(()), dma((edges // PAIR,))],
+        + [dma(()), dma((edges // STEP,))],
         compiler_params=pltpu.CompilerParams(vmem_limit_bytes=24 * 1024 * 1024),
         name="mesh_second",
     )(*between)

time: 20.8 us -> 20.8 us (level)
  no operation moved by 1% of the time
where the time goes in v4:
time: 20.8 us; the launch traced here: 20.7 us
  Pallas kernels  19.9 us (96%)
  between operations  0.81 us (4%)
    pallas_call x1, Pallas kernels, local(): pl.pallas_call(functools.partial(first_entry, n_row, n_col), out_shape=tu...  15.9 us
    pallas_call x1, Pallas kernels, local(): pl.pallas_call(second_entry, out_shape=tuple(shared), in_specs=[vmem] * l...  4 us

profile of v4, /device:TPU:0, one launch (start us, length us, event | category | flops | bytes accessed | tf_op | source)
XLA Modules:
  0.0 20.7 jit_solution(16562077308959787297)
XLA Ops:
  0.6 15.9 %mesh_first.1 = (bf16[1024,128]{1,0:T(8,128)(2,1)S(1)}, bf16[4096,128]{1,0:T(8,128)(2,1)S(1)}, f32[4096,128]{1,0:T(8,128)S(1)}, f32[4096,128]{1,0:T(8,128)S(1)},...) custom-call(bf16[1024,128]{1,0:T(8,128)(2,1)} %refs_0_.1, ...), custom_call_target="tpu_custom_call" | custom-call | tf_op jit(solution)/shard_map/mesh_first/pallas_call | solution.py:667
  16.5 4.0 %mesh_second.1 = (bf16[1024,128]{1,0:T(8,128)(2,1)}, bf16[4096,128]{1,0:T(8,128)(2,1)}) custom-call(bf16[1024,128]{1,0:T(8,128)(2,1)S(1)} %get-tuple-element.18.refs_0_, bf16[4096,128]{1,0:T(8,128)(2,1)S(1)} %get-tuple-element.19.refs_1_, f32[4096,128]{1,0:T(8,128)S(1)} %get-tuple-element.20.refs_2_, f32[4096,128]{1,0:T(8,128)S(1)} %get-tuple-element.21.refs_3_, ...), custom_call_target="tpu_custom_call" | custom-call | tf_op jit(solution)/shard_map/mesh_second/pallas_call | solution.py:703
